TPU v7x, 32 devices: a whole 2x2x4 slice. The times are simulated.
32 devices in a mesh: rows: 8 (over y, x, core), planes: 4 (over z).
Axes of the slice: x: 2, y: 2, z: 4, core: 2. Of those that a mesh axis runs over, the one named last changes fastest.
Arguments:
- density: float32 [4, 4096, 4096], P('planes', 'rows'), may hold values from -6 to 6
- lens_weight: float32 [4], P('planes'), may hold values from 0.05 to 0.5
- spectrum_bin: int32 [4096, 4096], P(None, ('rows', 'planes')), may hold values from 0 to 63, as said below
Outputs:
- shear_real: float32 [4096, 4096], P(('rows', 'planes'))
- shear_imag: float32 [4096, 4096], P(('rows', 'planes'))
- spectrum: float32 [64], replicated
Inputs may be any that keep to these rules, and one draw needn't show every extreme that they name: `spectrum_bin`: each Fourier pixel's band.
All inputs are finite; a program needn't handle non-finite values.
Results may differ from a plain program's by a relative error of at most 0.0003.
Values sent between devices are 32-bit elements; how exact they have to be, the bound alone decides.
A program may use at most 64 MiB of HBM per device.

v0:
```python
import functools
import math

import jax
import jax.numpy as jnp
import numpy as np
from jax import lax
from jax.experimental import pallas as pl
from jax.experimental.pallas import tpu as pltpu
from jax.sharding import PartitionSpec as P

NBINS = 64
AXES = ("rows", "planes")
LANES = 128
HALF = LANES // 2
TILE = 8
MESH = pl.DeviceIdType.MESH
F32 = jnp.float32
BF16 = jnp.bfloat16


def real_fft(xs):
    n = len(xs)
    if n == 2:
        return [(xs[0] + xs[1], None), (xs[0] - xs[1], None)]
    even, odd = real_fft(xs[0::2]), real_fft(xs[1::2])
    out = [None] * (n // 2 + 1)
    out[0] = (even[0][0] + odd[0][0], None)
    out[n // 2] = (even[0][0] - odd[0][0], None)
    out[n // 4] = (even[n // 4][0], -odd[n // 4][0])
    for k in range(1, n // 4):
        c, s = math.cos(2 * math.pi * k / n), math.sin(2 * math.pi * k / n)
        (er, ei), (odr, odi) = even[k], odd[k]
        tr, ti = c * odr + s * odi, c * odi - s * odr
        out[k] = (er + tr, ei + ti)
        out[n // 2 - k] = (er - tr, ti - ei)
    return out


def real_inverse(spec, n):
    if n == 2:
        return [spec[0][0] + spec[1][0], spec[0][0] - spec[1][0]]
    h, q = n // 2, n // 4
    even, odd = [None] * (q + 1), [None] * (q + 1)
    even[0] = (spec[0][0] + spec[h][0], None)
    odd[0] = (spec[0][0] - spec[h][0], None)
    even[q] = (2.0 * spec[q][0], None)
    odd[q] = (-2.0 * spec[q][1], None)
    for k in range(1, q):
        (ar, ai), (br, bi) = spec[k], spec[h - k]
        even[k] = (ar + br, ai - bi)
        ur, ui = ar - br, ai + bi
        c, s = math.cos(2 * math.pi * k / n), math.sin(2 * math.pi * k / n)
        odd[k] = (c * ur - s * ui, c * ui + s * ur)
    evens, odds = real_inverse(even, h), real_inverse(odd, h)
    out = [None] * n
    out[0::2], out[1::2] = evens, odds
    return out


def packed_fft(xs, orient, times_i):
    n = len(xs)
    if n == 1:
        return xs
    even = packed_fft(xs[0::2], orient, times_i)
    odd = packed_fft(xs[1::2], orient, times_i)
    out = [None] * n
    for k in range(n // 2):
        c, s = math.cos(2 * math.pi * k / n), orient * math.sin(2 * math.pi * k / n)
        if k == 0:
            t = odd[0]
        elif 4 * k == n:
            t = times_i(odd[k]) * float(orient)
        else:
            t = c * odd[k] + s * times_i(odd[k])
        out[k], out[k + n // 2] = even[k] + t, even[k] - t
    return out


def split(x):
    high = x.astype(BF16)
    return high, (x - high.astype(F32)).astype(BF16)


def dot3(left, right):
    lh, ll = split(left)
    rh, rl = split(right)
    return jnp.dot(
        jnp.concatenate([lh, lh, ll], 1),
        jnp.concatenate([rh, rl, rh], 0),
        preferred_element_type=F32,
    )


def row_tables(fold):
    length = fold * LANES
    a = np.arange(LANES)
    general = np.zeros((2, LANES, 2, 2, HALF))
    special = np.zeros((2, LANES, 2, 2, HALF))
    for h in range(2):
        m = h * HALF + np.arange(HALF)
        angle = 2 * np.pi * (a[:, None] * m[None, :] % LANES) / LANES
        general[0, :, h, 0], general[0, :, h, 1] = np.cos(angle), -np.sin(angle)
        general[1, :, h, 0], general[1, :, h, 1] = np.sin(angle), np.cos(angle)
        kx = fold * np.arange(HALF) + h * (fold // 2)
        angle = 2 * np.pi * (a[:, None] * kx[None, :] % length) / length
        special[h, :, h, 0], special[h, :, h, 1] = np.cos(angle), -np.sin(angle)
    special[0, :, 0, 1, 0] = 1 - 2 * (a % 2)
    shape = (2 * LANES, 2 * LANES)
    return general.reshape(shape).astype(np.float32), special.reshape(shape).astype(np.float32)


def back_tables(fold):
    length = fold * LANES
    a = np.arange(LANES)
    general = np.zeros((2, 2, HALF, 2, LANES))
    special = np.zeros((2, 2, HALF, 2, LANES))
    for h in range(2):
        m = h * HALF + np.arange(HALF)
        angle = 2 * np.pi * (m[:, None] * a[None, :] % LANES) / LANES
        general[h, 0, :, 0], general[h, 0, :, 1] = np.cos(angle), np.sin(angle)
        general[h, 1, :, 0], general[h, 1, :, 1] = -np.sin(angle), np.cos(angle)
        kx = fold * np.arange(HALF) + h * (fold // 2)
        angle = 2 * np.pi * (kx[:, None] * a[None, :] % length) / length
        special[h, 0, :, h], special[h, 1, :, h] = 2 * np.cos(angle), -2 * np.sin(angle)
    special[0, 0, 0, 0] = 1.0
    special[0, 1, 0, 0] = 1 - 2 * (a % 2)
    shape, scale = (2 * LANES, 2 * LANES), float(length) ** -2
    return (
        (general.reshape(shape) * scale).astype(np.float32),
        (special.reshape(shape) * scale).astype(np.float32),
    )


def column_table():
    a = np.arange(LANES)
    angle = 2 * np.pi * (a[:, None] * a[None, :] % LANES) / LANES
    return np.concatenate([np.cos(angle), np.sin(angle)], 1).astype(np.float32)


def turn_table(length):
    angle = 2 * np.pi * np.arange(LANES)[:, None] / length * np.ones((1, LANES))
    return np.stack([np.cos(angle), np.sin(angle)]).astype(np.float32)


def shear_kernel(
    rows, planes, slab,
    density, weight, bins, row_base, row_zero, back_base, back_zero, column, turns,
    out_real, out_imag, out_spectrum,
    staged, folded, parts, from_low, from_high, lines, hat, shear, power, arrived,
    bins_in, bands, sums, sums_out, sums_in, table,
    stage_sem, low_send, low_recv, high_send, high_recv, cross_send, cross_recv,
    bins_send, bins_recv, bins_own, turn_send, turn_recv, sum_send, sum_recv,
):
    devices = rows * planes
    fold = devices
    length = fold * LANES
    slots = fold // 2
    blocks = slab // LANES
    pairs = planes // 2
    angle_unit = 2 * math.pi / length
    r, p = lax.axis_index("rows"), lax.axis_index("planes")
    me = r * planes + p

    def place(device):
        return {"rows": device // planes, "planes": lax.rem(device, planes)}

    lane = lax.broadcasted_iota(jnp.int32, (1, LANES), 1)
    sign = jnp.where(lane < HALF, -1.0, 1.0)

    def times_i(x):
        return pltpu.roll(x, HALF, axis=1) * sign

    def minus_i(x):
        return pltpu.roll(x, HALF, axis=1) * (-sign)

    barrier = pltpu.get_barrier_semaphore()
    for step in range(1, devices):
        pl.semaphore_signal(
            barrier, inc=1, device_id=place(lax.rem(me + step, devices)), device_id_type=MESH
        )

    depth = staged.shape[1]
    chunks = slab // depth

    def stage(c):
        slot = lax.rem(c, 2)
        return pltpu.make_async_copy(
            density.at[pl.ds(c * depth, depth)], staged.at[slot], stage_sem.at[slot]
        )

    stage(0).start()
    scale = weight[0]

    def stage_step(c, carry):
        @pl.when(c + 1 < chunks)
        def _():
            stage(c + 1).start()

        stage(c).wait()
        slot = lax.rem(c, 2)

        def tile(i, carry):
            take = pl.ds(pl.multiple_of(i * TILE, TILE), TILE)
            xs = [staged[slot, take, b * LANES:(b + 1) * LANES] * scale for b in range(fold)]
            spec = real_fft(xs)
            put = pl.ds(pl.multiple_of(c * depth + i * TILE, TILE), TILE)
            folded[0, put, :LANES] = spec[0][0]
            folded[0, put, LANES:] = spec[slots][0]
            for k in range(1, slots):
                folded[k, put, :LANES] = spec[k][0]
                folded[k, put, LANES:] = spec[k][1]
            return carry

        return lax.fori_loop(0, depth // TILE, tile, carry)

    lax.fori_loop(0, chunks, stage_step, 0)
    pl.semaphore_wait(barrier, devices - 1)

    def up(dest, owner):
        return pltpu.make_async_remote_copy(
            parts.at[dest, owner], from_low.at[dest, owner - 1],
            low_send.at[dest, owner - 1], low_recv.at[dest, owner - 1],
            device_id={"rows": r, "planes": lax.rem(p + 1, planes)}, device_id_type=MESH,
        )

    def down(dest, owner):
        return pltpu.make_async_remote_copy(
            parts.at[dest, owner], from_high.at[dest, owner],
            high_send.at[dest, owner], high_recv.at[dest, owner],
            device_id={"rows": r, "planes": lax.rem(p + planes - 1, planes)},
            device_id_type=MESH,
        )

    def cross(dest):
        return pltpu.make_async_remote_copy(
            parts.at[dest, p], lines.at[pl.ds(r * blocks, blocks)],
            cross_send.at[dest], cross_recv.at[r],
            device_id={"rows": dest, "planes": p}, device_id_type=MESH,
        )

    def crossed(source):
        return pltpu.make_async_remote_copy(
            parts.at[source, p], lines.at[pl.ds(source * blocks, blocks)],
            cross_send.at[source], cross_recv.at[source],
            device_id={"rows": source, "planes": p}, device_id_type=MESH,
        )

    at_a = lax.broadcasted_iota(jnp.int32, (LANES, LANES), 0)

    def row_step(i, carry):
        dest = lax.rem(r + 1 + i, rows)
        for pair in range(pairs):
            k = dest * pairs + pair
            angle = (at_a * k).astype(F32) * angle_unit
            c, s = jnp.cos(angle), jnp.sin(angle)
            c, s = jnp.concatenate([c, c], 1), jnp.concatenate([s, s], 1)
            top, low = row_base[:LANES], row_base[LANES:]
            table[:LANES] = c * top - s * low
            table[LANES:] = c * low + s * top

            @pl.when(k == 0)
            def _():
                table[...] = row_zero[...]

            right = table[...]
            for q in range(blocks):
                done = dot3(folded[k, q * LANES:(q + 1) * LANES], right)
                parts[dest, 2 * pair, q] = done[:, :LANES]
                parts[dest, 2 * pair + 1, q] = done[:, LANES:]

        @pl.when(p == 0)
        def _():
            for owner in range(planes - 1, 0, -1):
                up(dest, owner).start()

        @pl.when(p == planes - 1)
        def _():
            for owner in range(planes - 1):
                down(dest, owner).start()

        return carry

    lax.fori_loop(0, rows, row_step, 0)

    side = me // slots

    def class_at(owner):
        k, h = owner // 2, lax.rem(owner, 2)
        other = k + lax.rem(h + side, 2) * (fold - 2 * k)
        return jnp.where(k == 0, h * slots, other)

    def send_bins(step):
        owner = lax.rem(me + step, devices)
        return pltpu.make_async_remote_copy(
            bins.at[class_at(owner)], bins_in.at[me],
            bins_send.at[step], bins_recv.at[step],
            device_id=place(owner), device_id_type=MESH,
        )

    def recv_bins(step):
        source = lax.rem(me + devices - step, devices)
        return pltpu.make_async_remote_copy(
            bins.at[0], bins_in.at[source],
            bins_send.at[step], bins_recv.at[step],
            device_id=place(source), device_id_type=MESH,
        )

    own_bins = pltpu.make_async_copy(bins.at[class_at(me)], bins_in.at[me], bins_own)
    own_bins.start()

    def bins_step(step, carry):
        send_bins(step).start()
        return carry

    lax.fori_loop(1, devices, bins_step, 0)

    def sum_step(i, carry):
        dest = lax.rem(r + 1 + i, rows)
        for back in range(planes - 1):
            owner = planes - 1 - back

            @pl.when((p >= 1) & (p <= owner))
            def _():
                up(dest, owner).wait_recv()
                parts[dest, owner] = parts[dest, owner] + from_low[dest, owner - 1]

            @pl.when((p >= 1) & (p < owner))
            def _():
                up(dest, owner).start()

            owner_down = back

            @pl.when((p <= planes - 2) & (p >= owner_down))
            def _():
                down(dest, owner_down).wait_recv()
                parts[dest, owner_down] = parts[dest, owner_down] + from_high[dest, owner_down]

            @pl.when((p <= planes - 2) & (p > owner_down))
            def _():
                down(dest, owner_down).start()

        @pl.when(dest != r)
        def _():
            cross(dest).start()

        return carry

    lax.fori_loop(0, rows, sum_step, 0)

    def own_step(q, carry):
        lines[r * blocks + q] = parts[r, p, q]
        return carry

    lax.fori_loop(0, blocks, own_step, 0)

    def crossed_step(i, carry):
        crossed(lax.rem(r + rows - 1 - i, rows)).wait_recv()
        return carry

    lax.fori_loop(0, rows - 1, crossed_step, 0)

    def column_tile(i, carry):
        take = pl.ds(pl.multiple_of(i * TILE, TILE), TILE)
        spec = packed_fft([lines[b, take] for b in range(fold)], -1, times_i)
        for k in range(fold):
            lines[k, take] = spec[k]
        return carry

    lax.fori_loop(0, LANES // TILE, column_tile, 0)

    k_me, h_me = me // 2, lax.rem(me, 2)
    index = lax.rem(lane, HALF)
    kx = jnp.where(
        k_me == 0, fold * index + h_me * slots, fold * (HALF * h_me + index) + k_me
    )
    across = jnp.where(kx >= length // 2, kx - length, kx).astype(F32)
    my = lax.broadcasted_iota(jnp.int32, (LANES, LANES), 0)
    at_lane = lax.broadcasted_iota(jnp.int32, (LANES, LANES), 1)
    pixel_scale = NBINS / float(length) ** 4

    def height_of(k):
        ky = k + fold * my
        return jnp.where(ky >= length // 2, ky - length, ky).astype(F32)

    def kernel_of(width, height):
        square_norm = height * height + width * width
        safe = jnp.where(square_norm == 0.0, 1.0, square_norm)
        inverse = 1.0 / safe
        return (width * width - height * height) * inverse, 2.0 * width * height * inverse

    def edge_of(k):
        return (my == HALF) & (k == 0)

    def column_step(k, carry):
        angle = (lane * k).astype(F32) * angle_unit
        c, s = jnp.cos(angle), jnp.sin(angle)
        cos, sin = column[:, :LANES], column[:, LANES:]
        left = jnp.concatenate([cos * c - sin * s, sin * c + cos * s], 1)
        z = lines[k]
        v = dot3(left, jnp.concatenate([z, minus_i(z)], 0))
        hat[k] = v
        square = v * v
        power[k] = (square + pltpu.roll(square, HALF, axis=1)) * pixel_scale
        kernel_real, kernel_imag = kernel_of(across, height_of(k))
        edge = edge_of(k)
        shear[k, :, :LANES] = kernel_real * v + jnp.where(edge, kernel_imag * times_i(v), 0.0)
        shear[k, :, LANES:] = jnp.where(edge, 0.0, kernel_imag * v)
        return carry

    lax.fori_loop(0, fold, column_step, 0)

    def reverse_of(k):
        wrapped = jnp.where(k == 0, LANES - my, LANES - 1 - my)
        return jnp.where(lax.rem(wrapped, LANES) == at_lane, 1.0, 0.0).astype(BF16)

    @pl.when(me == 0)
    def _():
        def repair(k, carry):
            v = hat[k]
            high, low = split(hat[lax.rem(fold - k, fold)])
            reverse = reverse_of(k)
            mirror = jnp.dot(reverse, high, preferred_element_type=F32) + jnp.dot(
                reverse, low, preferred_element_type=F32
            )
            mirror = mirror * (-sign)
            zero = (v + mirror) * 0.5
            zero = jnp.where((my == 0) & (k == 0), 0.0, zero)
            last = minus_i((v - mirror) * 0.5)
            zero_square, last_square = zero * zero, last * last
            zero_power = (zero_square + pltpu.roll(zero_square, HALF, axis=1)) * pixel_scale
            last_power = (last_square + pltpu.roll(last_square, HALF, axis=1)) * pixel_scale
            held = jnp.where(at_lane == HALF, last_power, power[k])
            power[k] = jnp.where(at_lane == 0, zero_power, held)
            height = height_of(k)
            kernel_real, kernel_imag = kernel_of(float(-(length // 2)), height)
            turned = times_i(kernel_real * last + kernel_imag * times_i(last))
            edge = edge_of(k)
            first = (at_lane == 0) | (at_lane == HALF)
            real = jnp.where(edge, 0.0, turned) - zero
            imag = jnp.where(edge, times_i(last), 0.0)
            shear[k, :, :LANES] = jnp.where(first, real, shear[k, :, :LANES])
            shear[k, :, LANES:] = jnp.where(first, imag, shear[k, :, LANES:])
            return carry

        lax.fori_loop(0, fold, repair, 0)

    table[:LANES] = column[...]

    def inverse_step(k, carry):
        real, imag = shear[k, :, :LANES], shear[k, :, LANES:]
        top = jnp.concatenate([real, imag], 1)
        low = jnp.concatenate([times_i(real), times_i(imag)], 1)
        shear[k] = dot3(table[:LANES], jnp.concatenate([top, low], 0))
        cos, sin = table[:LANES, :LANES], table[:LANES, LANES:]
        c, s = turns[0], turns[1]
        table[:LANES, :LANES] = cos * c - sin * s
        table[:LANES, LANES:] = sin * c + cos * s
        return carry

    lax.fori_loop(0, fold, inverse_step, 0)

    def inverse_tile(i, carry):
        take = pl.ds(pl.multiple_of(i * TILE, TILE), TILE)
        for part in range(2):
            span = slice(part * LANES, (part + 1) * LANES)
            lines_out = packed_fft([shear[k, take, span] for k in range(fold)], 1, times_i)
            for b in range(fold):
                shear[b, take, span] = lines_out[b]
        return carry

    lax.fori_loop(0, LANES // TILE, inverse_tile, 0)

    def give(step):
        dest = lax.rem(me + step, devices)
        return pltpu.make_async_remote_copy(
            shear.at[dest], arrived.at[me], turn_send.at[step], turn_recv.at[step],
            device_id=place(dest), device_id_type=MESH,
        )

    def got(step):
        source = lax.rem(me + devices - step, devices)
        return pltpu.make_async_remote_copy(
            shear.at[source], arrived.at[source], turn_send.at[step], turn_recv.at[step],
            device_id=place(source), device_id_type=MESH,
        )

    def give_step(step, carry):
        give(step).start()
        return carry

    lax.fori_loop(1, devices, give_step, 0)
    arrived[me] = shear[me]

    own_bins.wait()

    def bins_wait(step, carry):
        recv_bins(step).wait_recv()
        return carry

    lax.fori_loop(1, devices, bins_wait, 0)

    at_row = lax.broadcasted_iota(jnp.int32, (2 * LANES, 2 * LANES), 0)
    at_column = lax.broadcasted_iota(jnp.int32, (2 * LANES, 2 * LANES), 1)
    which = lax.rem(at_row // 4, 2)
    order = 4 * (at_row // 8) + lax.rem(at_row, 4)
    swapped = jnp.where(k_me == 0, 0, h_me)
    plain = lax.rem(1 - order // HALF + swapped, 2)
    origin = jnp.where((k_me == 0) & (h_me == 0), 2 * HALF, 2 * HALF - 1)
    inside = lax.rem(order, HALF)
    target = jnp.where(plain == 1, inside, HALF + lax.rem(origin - inside, HALF))
    target = target + which * LANES
    table[...] = jnp.where(target == at_column, 1.0, 0.0)

    def bins_turn(k, carry):
        block = bins_in[:, k].reshape(2 * LANES, LANES).astype(BF16)
        out = lax.dot_general(
            block, table[...].astype(BF16), (((0,), (0,)), ((), ())),
            preferred_element_type=F32,
        )
        bands[2 * k] = out[:, :LANES]
        bands[2 * k + 1] = out[:, LANES:]
        return carry

    lax.fori_loop(0, fold // 2, bins_turn, 0)
    sums[...] = jnp.zeros_like(sums)

    def band_step(k, carry):
        flipped = jnp.dot(
            reverse_of(k), bands[lax.rem(fold - k, fold)].astype(BF16),
            preferred_element_type=F32,
        )
        band = jnp.where(lane < HALF, bands[k], flipped)
        energy = power[k]
        for b in range(NBINS):
            kept = jnp.where(band == float(b), energy, 0.0)
            sums[b] += jnp.sum(kept.reshape(LANES // TILE, TILE, LANES), axis=0)
        return carry

    lax.fori_loop(0, fold, band_step, 0)
    totals = jnp.sum(jnp.sum(sums[...], axis=1), axis=1, keepdims=True)
    diagonal = lax.broadcasted_iota(jnp.int32, (NBINS, LANES), 0) == lax.broadcasted_iota(
        jnp.int32, (NBINS, LANES), 1
    )
    line = jnp.sum(jnp.where(diagonal, totals, 0.0), axis=0, keepdims=True)
    sums_out[...] = jnp.broadcast_to(line, (TILE, LANES))
    sums_in[me] = jnp.broadcast_to(line, (TILE, LANES))

    def tell(step):
        dest = lax.rem(me + step, devices)
        return pltpu.make_async_remote_copy(
            sums_out, sums_in.at[me], sum_send.at[step], sum_recv.at[step],
            device_id=place(dest), device_id_type=MESH,
        )

    def told(step):
        source = lax.rem(me + devices - step, devices)
        return pltpu.make_async_remote_copy(
            sums_out, sums_in.at[source], sum_send.at[step], sum_recv.at[step],
            device_id=place(source), device_id_type=MESH,
        )

    def tell_step(step, carry):
        tell(step).start()
        return carry

    lax.fori_loop(1, devices, tell_step, 0)

    def got_step(step, carry):
        got(step).wait_recv()
        return carry

    lax.fori_loop(1, devices, got_step, 0)

    def back_step(k, carry):
        angle = (lane * k).astype(F32) * angle_unit
        c, s = jnp.cos(angle), jnp.sin(angle)
        cos, sin = back_base[:, :LANES], back_base[:, LANES:]
        table[:, :LANES] = cos * c - sin * s
        table[:, LANES:] = sin * c + cos * s

        @pl.when(k == 0)
        def _():
            table[...] = back_zero[...]

        left = [
            jnp.concatenate(
                [arrived[2 * k + h, :, part * LANES:(part + 1) * LANES] for h in range(2)], 1
            )
            for part in range(2)
        ]
        folded[k, :2 * LANES] = dot3(jnp.concatenate(left, 0), table[...])
        return carry

    lax.fori_loop(0, slots, back_step, 0)

    for part, out in enumerate((out_real, out_imag)):
        def back_tile(i, carry, part=part, out=out):
            take = pl.ds(pl.multiple_of(part * LANES + i * TILE, TILE), TILE)
            spec = [(folded[0, take, :LANES], None)]
            for k in range(1, slots):
                spec.append((folded[k, take, :LANES], folded[k, take, LANES:]))
            spec.append((folded[0, take, LANES:], None))
            put = pl.ds(pl.multiple_of(i * TILE, TILE), TILE)
            for b, value in enumerate(real_inverse(spec, fold)):
                out[put, b * LANES:(b + 1) * LANES] = value
            return carry

        lax.fori_loop(0, LANES // TILE, back_tile, 0)

    def told_step(step, carry):
        told(step).wait_recv()
        return carry

    lax.fori_loop(1, devices, told_step, 0)
    out_spectrum[...] = jnp.sum(sums_in[...], axis=0)

    def last_step(step, carry):
        give(step).wait_send()
        tell(step).wait_send()
        send_bins(step).wait_send()
        return carry

    lax.fori_loop(1, devices, last_step, 0)

    def sent_step(dest, carry):
        for owner in range(planes):
            if owner > 0:
                @pl.when(p < owner)
                def _():
                    up(dest, owner).wait_send()

            if owner < planes - 1:
                @pl.when(p > owner)
                def _():
                    down(dest, owner).wait_send()

        @pl.when(dest != r)
        def _():
            cross(dest).wait_send()

        return carry

    lax.fori_loop(0, rows, sent_step, 0)


def folded_device(density, lens_weight, spectrum_bin):
    rows, planes = lax.axis_size("rows"), lax.axis_size("planes")
    devices = rows * planes
    slab, length = density.shape[1:]
    fold, blocks, slots = devices, slab // LANES, devices // 2
    groups = LANES // fold
    bins = spectrum_bin.reshape(LANES, fold // 2, 2, groups, fold)
    bins = bins.transpose(4, 1, 2, 3, 0).reshape(fold, fold // 2, 2 * groups, LANES)
    bins = bins.astype(F32)
    row_base, row_zero = row_tables(fold)
    back_base, back_zero = back_tables(fold)
    vmem = pl.BlockSpec(memory_space=pltpu.VMEM)
    hbm = pl.BlockSpec(memory_space=pl.ANY)
    smem = pl.BlockSpec(memory_space=pltpu.SMEM)
    dma = pltpu.SemaphoreType.DMA
    chunk = (blocks, LANES, LANES)
    scratch = [
        pltpu.VMEM((2, min(64, slab), length), F32),
        pltpu.VMEM((slots, slab, 2 * LANES), F32),
        pltpu.VMEM((rows, planes) + chunk, F32),
        pltpu.VMEM((rows, planes - 1) + chunk, F32),
        pltpu.VMEM((rows, planes - 1) + chunk, F32),
        pltpu.VMEM((fold, LANES, LANES), F32),
        pltpu.VMEM((fold, LANES, LANES), F32),
        pltpu.VMEM((fold, LANES, 2 * LANES), F32),
        pltpu.VMEM((fold, LANES, LANES), F32),
        pltpu.VMEM((devices, LANES, 2 * LANES), F32),
        pltpu.VMEM((devices, fold // 2, 2 * groups, LANES), F32),
        pltpu.VMEM((fold, LANES, LANES), F32),
        pltpu.VMEM((NBINS, TILE, LANES), F32),
        pltpu.VMEM((TILE, LANES), F32),
        pltpu.VMEM((devices, TILE, LANES), F32),
        pltpu.VMEM((2 * LANES, 2 * LANES), F32),
        dma((2,)),
        dma((rows, planes - 1)), dma((rows, planes - 1)),
        dma((rows, planes - 1)), dma((rows, planes - 1)),
        dma((rows,)), dma((rows,)),
        dma((devices,)), dma((devices,)), dma,
        dma((devices,)), dma((devices,)),
        dma((devices,)), dma((devices,)),
    ]
    real, imag, spectrum = pl.pallas_call(
        functools.partial(shear_kernel, rows, planes, slab),
        out_shape=(
            jax.ShapeDtypeStruct((length // devices, length), F32),
            jax.ShapeDtypeStruct((length // devices, length), F32),
            jax.ShapeDtypeStruct((TILE, LANES), F32),
        ),
        in_specs=[hbm, smem, hbm] + [vmem] * 6,
        out_specs=(vmem, vmem, vmem),
        scratch_shapes=scratch,
        compiler_params=pltpu.CompilerParams(
            collective_id=0, has_side_effects=True, vmem_limit_bytes=67043328
        ),
        name="shear",
    )(
        density[0], lens_weight, bins,
        row_base, row_zero, back_base, back_zero, column_table(), turn_table(length),
    )
    return real, imag, spectrum[0, :NBINS]


def phase(left, right, length, orient):
    index = np.arange(left)[:, None] * np.arange(right)[None, :] % length
    return np.exp(orient * 2j * math.pi * index / length)


def as_blocks(table):
    rows = np.stack([table.real, -table.imag], -1), np.stack([table.imag, table.real], -1)
    return np.stack(rows, 1).astype(np.float32)


def lane_table(table):
    top = np.concatenate([table.real, table.imag], 1)
    bottom = np.concatenate([-table.imag, table.real], 1)
    return np.concatenate([top, bottom], 0).astype(np.float32)


def product(pattern, left, right):
    return jnp.einsum(pattern, left, right, precision=lax.Precision.HIGH)


def turn(real, imag, table):
    cos, sin = table.real.astype(np.float32), table.imag.astype(np.float32)
    return real * cos - imag * sin, real * sin + imag * cos


def centred(indices, length):
    return ((indices + length // 2) % length - length // 2).astype(jnp.float32)


def plane_sum(density, lens_weight):
    count = lax.axis_size("planes")
    here = lax.axis_index("planes")
    block = density.shape[1] // count
    half = block // 2

    def own(owner, part):
        start = (owner % count) * block + part * half
        piece = lax.dynamic_slice_in_dim(density, start, half, axis=1)
        return jnp.sum(piece * lens_weight[:, None, None], axis=0)

    ways = ((0, 1), (1, -1))
    held = [own(here - way + count, part) for part, way in ways]
    for step in range(count - 1):
        moved = [
            lax.ppermute(held[part], "planes", [(i, (i + way) % count) for i in range(count)])
            for part, way in ways
        ]
        held = [
            moved[part] + own(here - way * (2 + step) + 2 * count, part) for part, way in ways
        ]
    return jnp.concatenate(held, axis=0)


def on_device(density, lens_weight, spectrum_bin):
    length = density.shape[-1]
    devices = lax.axis_size("rows") * lax.axis_size("planes")
    narrow = length // devices
    me = lax.axis_index("rows") * lax.axis_size("planes") + lax.axis_index("planes")

    share = plane_sum(density, lens_weight)
    field = share.T.reshape(narrow, devices, narrow)
    first = phase(narrow, narrow, narrow, -1)
    real = product("kn,nqy->kqy", first.real.astype(np.float32), field)
    imag = product("kn,nqy->kqy", first.imag.astype(np.float32), field)
    real, imag = turn(real, imag, phase(narrow, devices, length, -1)[:, :, None])
    forward = as_blocks(phase(devices, devices, devices, -1))
    spread = product("leq,kqy->leky", forward[..., 0], real) + product(
        "leq,kqy->leky", forward[..., 1], imag
    )
    held = lax.all_to_all(spread, AXES, split_axis=0, concat_axis=0, tiled=True)

    held = product("kesc,scxt->kext", forward, held)
    real, imag = turn(held[:, 0], held[:, 1], phase(devices, narrow, length, -1)[:, None, :])
    hat = product(
        "kxt,tm->kxm",
        jnp.concatenate([real, imag], -1),
        lane_table(phase(narrow, narrow, narrow, -1)),
    )
    hat_real, hat_imag = hat[..., :narrow], hat[..., narrow:]

    ky_index = (
        jnp.arange(devices, dtype=jnp.int32)[:, None, None]
        + devices * jnp.arange(narrow, dtype=jnp.int32)[None, None, :]
    )
    height = centred(ky_index, length)
    across = centred(me * narrow + jnp.arange(narrow, dtype=jnp.int32), length)[None, :, None]
    square_norm = height**2 + across**2
    anchor = square_norm == 0
    safe_norm = jnp.where(anchor, 1.0, square_norm)
    hat_real = jnp.where(anchor, 0.0, hat_real)
    hat_imag = jnp.where(anchor, 0.0, hat_imag)

    kernel_real = (across**2 - height**2) / safe_norm
    kernel_imag = 2.0 * across * height / safe_norm
    shear = jnp.concatenate(
        [
            kernel_real * hat_real - kernel_imag * hat_imag,
            kernel_real * hat_imag + kernel_imag * hat_real,
        ],
        -1,
    )
    back = product(
        "kxm,mt->kxt", shear, lane_table(phase(narrow, narrow, narrow, 1) / length)
    )
    real, imag = turn(
        back[..., :narrow], back[..., narrow:], phase(devices, narrow, length, 1)[:, None, :]
    )
    inverse = as_blocks(phase(devices, devices, devices, 1))
    back = product("sek,kxt->sext", inverse[..., 0], real) + product(
        "sek,kxt->sext", inverse[..., 1], imag
    )
    turned = lax.all_to_all(back, AXES, split_axis=0, concat_axis=0, tiled=True)

    pixel_power = (hat_real**2 + hat_imag**2) * (NBINS / float(length) ** 4)
    bins = spectrum_bin.reshape(narrow, devices, narrow).transpose(1, 2, 0)
    band_ids = jnp.arange(NBINS, dtype=jnp.int32)[:, None, None, None]
    partial_power = jnp.sum(jnp.where(bins == band_ids, pixel_power, 0.0), axis=(1, 2, 3))
    copies = jnp.broadcast_to(partial_power, (devices, 8, NBINS))
    gathered = lax.all_to_all(copies, AXES, split_axis=0, concat_axis=0, tiled=True)
    spectrum = jnp.sum(gathered[:, 0, :], axis=0)

    turned = product("aedc,dcqt->aeqt", inverse, turned)
    real, imag = turn(
        turned[:, 0], turned[:, 1], phase(devices, narrow, length, 1)[:, :, None]
    )
    last = phase(narrow, narrow, narrow, 1) / length
    cos, sin = last.real.astype(np.float32), last.imag.astype(np.float32)
    out_real = product("bq,aqt->bat", cos, real) - product("bq,aqt->bat", sin, imag)
    out_imag = product("bq,aqt->bat", sin, real) + product("bq,aqt->bat", cos, imag)
    shape = (length, narrow)
    return (out_real.reshape(shape).T, out_imag.reshape(shape).T, spectrum)


def folds(mesh, density):
    rows, planes = mesh.shape["rows"], mesh.shape["planes"]
    count, length, width = density.shape
    return (
        count == planes
        and planes % 2 == 0
        and planes >= 2
        and length == width == LANES * rows * planes
        and rows * planes == LANES // 4
    )


def solution(mesh):
    specs = (P("planes", "rows", None), P("planes"), P(None, AXES))
    outs = (P(AXES, None), P(AXES, None), P())

    def run(density, lens_weight, spectrum_bin):
        if folds(mesh, density):
            body = folded_device
        else:
            body = on_device
        whole = jax.shard_map(body, mesh=mesh, in_specs=specs, out_specs=outs, check_vma=False)
        return whole(density, lens_weight, spectrum_bin)

    return run
```

profile of v0, /device:TPU:25, one launch (start us, length us, event | category | flops | bytes accessed | tf_op | source)
XLA Modules:
  0.0 401.8 jit_solution(2425148318565512863)
XLA Ops:
  0.6 1.7 convert_element_type.9
  2.4 5.5 %convert_element_type.10 = f32[128,16,2,4,32]{4,3,2,1,0:T(4,128)} reshape(f32[4096,128]{1,0:T(8,128)S(1)} %convert_element_type.9) | data formatting | bytes 4194304 | tf_op jit(solution)/shard_map/convert_element_type | solution.py:655
  7.8 8.6 %copy.13 = f32[32,16,2,4,128]{4,3,2,1,0:T(4,128)} copy(f32[32,16,2,4,128]{0,3,2,1,4:T(4,128)} %bitcast.5) | data formatting | bytes 4194304 | tf_op jit(solution)/shard_map/convert_element_type | solution.py:655
  17.1 378.9 %shear.1 = (f32[128,4096]{1,0:T(8,128)}, f32[128,4096]{1,0:T(8,128)}, f32[8,128]{1,0:T(8,128)}) custom-call(f32[512,4096]{1,0:T(8,128)} %bitcast.6, f32[1]{0:T(128)S(6)} %copy.16.weight, f32[32,16,8,128]{3,2,1,0:T(8,128)} %bitcast.7, f32[256,256]{1,0:T(8,128)} %constant.12.clone.row_base, f32[256,256]{1,0:T(8,128)} %constant.13.clone.row_zero, ...), custom_call_target="tpu_custom_call" | custom-call | tf_op jit(solution)/shard_map/shear/pallas_call | solution.py:688
  396.0 1.2 slice_bitcast_fusion
  397.2 0.0 copy-start
  397.2 3.3 copy.17
  400.4 0.0 copy-done
  400.4 1.3 copy.18
Async XLA Ops:
  397.2 3.3 copy-start
where the time goes:
time: 402 us
  Pallas kernels  379 us (94%)
  local copies, waits for them, and re-layouts  19.8 us (5%)
    pallas_call x1, Pallas kernels, folded_device(): pl.pallas_call(functools.partial(shear_kernel, rows, planes, slab), out_s...  379 us
    convert_element_type x2, local copies, waits for them, and re-layouts, folded_device(): bins = bins.astype(F32)  14 us

commit v1 on v0

--- a/solution.py
+++ b/solution.py
@@ -58,21 +58,21 @@
     return out
 
 
-def packed_fft(xs, orient, times_i):
+def packed_fft(xs, orient, swap, sign):
     n = len(xs)
     if n == 1:
         return xs
-    even = packed_fft(xs[0::2], orient, times_i)
-    odd = packed_fft(xs[1::2], orient, times_i)
+    even = packed_fft(xs[0::2], orient, swap, sign)
+    odd = packed_fft(xs[1::2], orient, swap, sign)
     out = [None] * n
     for k in range(n // 2):
         c, s = math.cos(2 * math.pi * k / n), orient * math.sin(2 * math.pi * k / n)
         if k == 0:
             t = odd[0]
         elif 4 * k == n:
-            t = times_i(odd[k]) * float(orient)
+            t = swap(odd[k]) * (orient * sign)
         else:
-            t = c * odd[k] + s * times_i(odd[k])
+            t = c * odd[k] + swap(odd[k]) * (s * sign)
         out[k], out[k + n // 2] = even[k] + t, even[k] - t
     return out
 
@@ -147,16 +147,17 @@
     rows, planes, slab,
     density, weight, bins, row_base, row_zero, back_base, back_zero, column, turns,
     out_real, out_imag, out_spectrum,
-    staged, folded, parts, from_low, from_high, lines, hat, shear, power, arrived,
-    bins_in, bands, sums, sums_out, sums_in, table,
-    stage_sem, low_send, low_recv, high_send, high_recv, cross_send, cross_recv,
-    bins_send, bins_recv, bins_own, turn_send, turn_recv, sum_send, sum_recv,
+    staged, folded, parts, far_low, far_high, near_low, near_high, lines, hat, shear, power,
+    arrived, bins_raw, bins_out, bins_in, bands, sums, sums_out, sums_in, table, split_column,
+    stage_sem, sum_send, sum_recv, cross_send, cross_recv,
+    bins_send, bins_recv, bins_load, turn_send, turn_recv, total_send, total_recv,
 ):
     devices = rows * planes
     fold = devices
     length = fold * LANES
     slots = fold // 2
     blocks = slab // LANES
+    middle = blocks // 2
     pairs = planes // 2
     angle_unit = 2 * math.pi / length
     r, p = lax.axis_index("rows"), lax.axis_index("planes")
@@ -165,20 +166,30 @@
     def place(device):
         return {"rows": device // planes, "planes": lax.rem(device, planes)}
 
+    def remote(source, target, send, recv, device):
+        return pltpu.make_async_remote_copy(
+            source, target, send, recv, device_id=place(device), device_id_type=MESH
+        )
+
     lane = lax.broadcasted_iota(jnp.int32, (1, LANES), 1)
     sign = jnp.where(lane < HALF, -1.0, 1.0)
 
+    def swap(x):
+        return pltpu.roll(x, HALF, axis=1)
+
     def times_i(x):
-        return pltpu.roll(x, HALF, axis=1) * sign
+        return swap(x) * sign
 
     def minus_i(x):
-        return pltpu.roll(x, HALF, axis=1) * (-sign)
+        return swap(x) * (-sign)
 
     barrier = pltpu.get_barrier_semaphore()
     for step in range(1, devices):
         pl.semaphore_signal(
             barrier, inc=1, device_id=place(lax.rem(me + step, devices)), device_id_type=MESH
         )
+    load_bins = pltpu.make_async_copy(bins, bins_raw, bins_load)
+    load_bins.start()
 
     depth = staged.shape[1]
     chunks = slab // depth
@@ -217,33 +228,34 @@
     lax.fori_loop(0, chunks, stage_step, 0)
     pl.semaphore_wait(barrier, devices - 1)
 
-    def up(dest, owner):
-        return pltpu.make_async_remote_copy(
-            parts.at[dest, owner], from_low.at[dest, owner - 1],
-            low_send.at[dest, owner - 1], low_recv.at[dest, owner - 1],
-            device_id={"rows": r, "planes": lax.rem(p + 1, planes)}, device_id_type=MESH,
-        )
-
-    def down(dest, owner):
-        return pltpu.make_async_remote_copy(
-            parts.at[dest, owner], from_high.at[dest, owner],
-            high_send.at[dest, owner], high_recv.at[dest, owner],
-            device_id={"rows": r, "planes": lax.rem(p + planes - 1, planes)},
-            device_id_type=MESH,
+    first, second = pl.ds(0, middle), pl.ds(middle, blocks - middle)
+    above, below = lax.rem(p + 1, planes), lax.rem(p + planes - 1, planes)
+    across_ring = lax.rem(p + 2, planes)
+
+    def sum_copy(which, dest):
+        owner, half, target, to = (
+            (across_ring, first, far_high.at[dest], below),
+            (across_ring, second, far_low.at[dest], above),
+            (above, first, near_low.at[dest, first], above),
+            (above, second, near_low.at[dest, second], above),
+            (below, first, near_high.at[dest, first], below),
+            (below, second, near_high.at[dest, second], below),
+        )[which]
+        return remote(
+            parts.at[dest, owner, half], target,
+            sum_send.at[which, dest], sum_recv.at[which, dest], r * planes + to,
         )
 
     def cross(dest):
-        return pltpu.make_async_remote_copy(
+        return remote(
             parts.at[dest, p], lines.at[pl.ds(r * blocks, blocks)],
-            cross_send.at[dest], cross_recv.at[r],
-            device_id={"rows": dest, "planes": p}, device_id_type=MESH,
+            cross_send.at[dest], cross_recv.at[r], dest * planes + p,
         )
 
     def crossed(source):
-        return pltpu.make_async_remote_copy(
+        return remote(
             parts.at[source, p], lines.at[pl.ds(source * blocks, blocks)],
-            cross_send.at[source], cross_recv.at[source],
-            device_id={"rows": source, "planes": p}, device_id_type=MESH,
+            cross_send.at[source], cross_recv.at[source], source * planes + p,
         )
 
     at_a = lax.broadcasted_iota(jnp.int32, (LANES, LANES), 0)
@@ -269,20 +281,29 @@
                 parts[dest, 2 * pair, q] = done[:, :LANES]
                 parts[dest, 2 * pair + 1, q] = done[:, LANES:]
 
-        @pl.when(p == 0)
-        def _():
-            for owner in range(planes - 1, 0, -1):
-                up(dest, owner).start()
-
-        @pl.when(p == planes - 1)
-        def _():
-            for owner in range(planes - 1):
-                down(dest, owner).start()
-
+        for which in (0, 1, 2, 5):
+            sum_copy(which, dest).start()
         return carry
 
     lax.fori_loop(0, rows, row_step, 0)
 
+    at_row = lax.broadcasted_iota(jnp.int32, (2 * LANES, 2 * LANES), 0)
+    at_column = lax.broadcasted_iota(jnp.int32, (2 * LANES, 2 * LANES), 1)
+    which_row = lax.rem(at_row // 4, 2)
+    target = which_row * LANES + lax.rem(at_row, 4) * fold + at_row // 8
+    table[...] = jnp.where(target == at_column, 1.0, 0.0)
+    load_bins.wait()
+
+    def bins_layout(k, carry):
+        both = [bins_raw[pl.ds(2 * k + q, LANES, stride=fold), :] for q in range(2)]
+        both = jnp.concatenate(both, 1).astype(F32).astype(BF16)
+        out = lax.dot_general(
+            table[...].astype(BF16), both, (((1,), (1,)), ((), ())), preferred_element_type=F32
+        )
+        bins_out[:, k] = out.reshape(fold, TILE, LANES)
+        return carry
+
+    lax.fori_loop(0, fold // 2, bins_layout, 0)
     side = me // slots
 
     def class_at(owner):
@@ -292,53 +313,41 @@
 
     def send_bins(step):
         owner = lax.rem(me + step, devices)
-        return pltpu.make_async_remote_copy(
-            bins.at[class_at(owner)], bins_in.at[me],
-            bins_send.at[step], bins_recv.at[step],
-            device_id=place(owner), device_id_type=MESH,
+        return remote(
+            bins_out.at[class_at(owner)], bins_in.at[me],
+            bins_send.at[step], bins_recv.at[step], owner,
         )
 
     def recv_bins(step):
         source = lax.rem(me + devices - step, devices)
-        return pltpu.make_async_remote_copy(
-            bins.at[0], bins_in.at[source],
-            bins_send.at[step], bins_recv.at[step],
-            device_id=place(source), device_id_type=MESH,
-        )
-
-    own_bins = pltpu.make_async_copy(bins.at[class_at(me)], bins_in.at[me], bins_own)
-    own_bins.start()
+        return remote(
+            bins_out.at[0], bins_in.at[source], bins_send.at[step], bins_recv.at[step], source
+        )
+
+    def relay_step(i, carry):
+        dest = lax.rem(r + 1 + i, rows)
+        sum_copy(1, dest).wait_recv()
+        parts[dest, above, second] = parts[dest, above, second] + far_low[dest]
+        sum_copy(3, dest).start()
+        sum_copy(0, dest).wait_recv()
+        parts[dest, below, first] = parts[dest, below, first] + far_high[dest]
+        sum_copy(4, dest).start()
+        return carry
+
+    lax.fori_loop(0, rows, relay_step, 0)
 
     def bins_step(step, carry):
         send_bins(step).start()
         return carry
 
     lax.fori_loop(1, devices, bins_step, 0)
-
-    def sum_step(i, carry):
+    bins_in[me] = bins_out[class_at(me)]
+
+    def owner_step(i, carry):
         dest = lax.rem(r + 1 + i, rows)
-        for back in range(planes - 1):
-            owner = planes - 1 - back
-
-            @pl.when((p >= 1) & (p <= owner))
-            def _():
-                up(dest, owner).wait_recv()
-                parts[dest, owner] = parts[dest, owner] + from_low[dest, owner - 1]
-
-            @pl.when((p >= 1) & (p < owner))
-            def _():
-                up(dest, owner).start()
-
-            owner_down = back
-
-            @pl.when((p <= planes - 2) & (p >= owner_down))
-            def _():
-                down(dest, owner_down).wait_recv()
-                parts[dest, owner_down] = parts[dest, owner_down] + from_high[dest, owner_down]
-
-            @pl.when((p <= planes - 2) & (p > owner_down))
-            def _():
-                down(dest, owner_down).start()
+        for which in (2, 3, 4, 5):
+            sum_copy(which, dest).wait_recv()
+        parts[dest, p] = parts[dest, p] + near_low[dest] + near_high[dest]
 
         @pl.when(dest != r)
         def _():
@@ -346,7 +355,7 @@
 
         return carry
 
-    lax.fori_loop(0, rows, sum_step, 0)
+    lax.fori_loop(0, rows, owner_step, 0)
 
     def own_step(q, carry):
         lines[r * blocks + q] = parts[r, p, q]
@@ -362,9 +371,13 @@
 
     def column_tile(i, carry):
         take = pl.ds(pl.multiple_of(i * TILE, TILE), TILE)
-        spec = packed_fft([lines[b, take] for b in range(fold)], -1, times_i)
-        for k in range(fold):
-            lines[k, take] = spec[k]
+        spec = packed_fft([lines[b, take] for b in range(fold)], -1, swap, sign)
+        lines[0, take] = spec[0]
+        c1, s1 = turns[0, take], turns[1, take] * sign
+        c, s = c1, s1
+        for k in range(1, fold):
+            lines[k, take] = spec[k] * c - swap(spec[k]) * s
+            c, s = c * c1 - s * s1, s * c1 + c * s1
         return carry
 
     lax.fori_loop(0, LANES // TILE, column_tile, 0)
@@ -392,107 +405,134 @@
     def edge_of(k):
         return (my == HALF) & (k == 0)
 
-    def column_step(k, carry):
-        angle = (lane * k).astype(F32) * angle_unit
-        c, s = jnp.cos(angle), jnp.sin(angle)
-        cos, sin = column[:, :LANES], column[:, LANES:]
-        left = jnp.concatenate([cos * c - sin * s, sin * c + cos * s], 1)
-        z = lines[k]
-        v = dot3(left, jnp.concatenate([z, minus_i(z)], 0))
-        hat[k] = v
-        square = v * v
-        power[k] = (square + pltpu.roll(square, HALF, axis=1)) * pixel_scale
-        kernel_real, kernel_imag = kernel_of(across, height_of(k))
-        edge = edge_of(k)
-        shear[k, :, :LANES] = kernel_real * v + jnp.where(edge, kernel_imag * times_i(v), 0.0)
-        shear[k, :, LANES:] = jnp.where(edge, 0.0, kernel_imag * v)
-        return carry
-
-    lax.fori_loop(0, fold, column_step, 0)
-
-    def reverse_of(k):
-        wrapped = jnp.where(k == 0, LANES - my, LANES - 1 - my)
-        return jnp.where(lax.rem(wrapped, LANES) == at_lane, 1.0, 0.0).astype(BF16)
+    high, low = split(column[...])
+    split_column[...] = jnp.concatenate([high, high, low], 1)
+
+    def column_product(right):
+        rh, rl = split(right)
+        return jnp.dot(
+            split_column[...], jnp.concatenate([rh, rl, rh], 0), preferred_element_type=F32
+        )
+
+    def each(f, x):
+        count = x.shape[1] // LANES
+        return jnp.concatenate([f(x[:, q * LANES:(q + 1) * LANES]) for q in range(count)], 1)
+
+    def column_step(j, carry):
+        z = jnp.concatenate([lines[2 * j], lines[2 * j + 1]], 1)
+        both = column_product(jnp.concatenate([z, each(minus_i, z)], 0))
+        turned = []
+        for q in range(2):
+            k = 2 * j + q
+            v = both[:, q * LANES:(q + 1) * LANES]
+            hat[k] = v
+            square = v * v
+            power[k] = (square + swap(square)) * pixel_scale
+            kernel_real, kernel_imag = kernel_of(across, height_of(k))
+            edge = edge_of(k)
+            turned += [
+                kernel_real * v + jnp.where(edge, kernel_imag * times_i(v), 0.0),
+                jnp.where(edge, 0.0, kernel_imag * v),
+            ]
+        turned = jnp.concatenate(turned, 1)
+        back = column_product(jnp.concatenate([turned, each(times_i, turned)], 0))
+        shear[2 * j] = back[:, :2 * LANES]
+        shear[2 * j + 1] = back[:, 2 * LANES:]
+        return carry
+
+    lax.fori_loop(0, fold // 2, column_step, 0)
+
+    def reverse_of(wrap):
+        return jnp.where(lax.rem(LANES - wrap - my, LANES) == at_lane, 1.0, 0.0).astype(BF16)
 
     @pl.when(me == 0)
     def _():
-        def repair(k, carry):
-            v = hat[k]
-            high, low = split(hat[lax.rem(fold - k, fold)])
-            reverse = reverse_of(k)
-            mirror = jnp.dot(reverse, high, preferred_element_type=F32) + jnp.dot(
-                reverse, low, preferred_element_type=F32
+        spot = lax.rem(at_lane, HALF)
+
+        def gather(k, held):
+            return jnp.where(spot == k, pltpu.roll(hat[k], k, axis=1), held)
+
+        v = lax.fori_loop(0, fold, gather, jnp.zeros((LANES, LANES), F32))
+        high, low = split(v)
+
+        def moved(wrap):
+            mover = reverse_of(wrap)
+            return jnp.dot(mover, high, preferred_element_type=F32) + jnp.dot(
+                mover, low, preferred_element_type=F32
             )
-            mirror = mirror * (-sign)
-            zero = (v + mirror) * 0.5
-            zero = jnp.where((my == 0) & (k == 0), 0.0, zero)
-            last = minus_i((v - mirror) * 0.5)
-            zero_square, last_square = zero * zero, last * last
-            zero_power = (zero_square + pltpu.roll(zero_square, HALF, axis=1)) * pixel_scale
-            last_power = (last_square + pltpu.roll(last_square, HALF, axis=1)) * pixel_scale
-            held = jnp.where(at_lane == HALF, last_power, power[k])
-            power[k] = jnp.where(at_lane == 0, zero_power, held)
-            height = height_of(k)
-            kernel_real, kernel_imag = kernel_of(float(-(length // 2)), height)
-            turned = times_i(kernel_real * last + kernel_imag * times_i(last))
-            edge = edge_of(k)
-            first = (at_lane == 0) | (at_lane == HALF)
-            real = jnp.where(edge, 0.0, turned) - zero
-            imag = jnp.where(edge, times_i(last), 0.0)
-            shear[k, :, :LANES] = jnp.where(first, real, shear[k, :, :LANES])
-            shear[k, :, LANES:] = jnp.where(first, imag, shear[k, :, LANES:])
+
+        my_spot = lax.rem(my, HALF)
+        same = (my // HALF == at_lane // HALF) & (spot < fold)
+        partner = jnp.where(same & (lax.rem(fold - spot, fold) == my_spot), 1.0, 0.0)
+        partner = partner.astype(BF16)
+        high, low = split(jnp.where(spot == 0, moved(0), moved(1)))
+        mirror = jnp.dot(high, partner, preferred_element_type=F32) + jnp.dot(
+            low, partner, preferred_element_type=F32
+        )
+        mirror = mirror * (-sign)
+        zero = jnp.where((my == 0) & (spot == 0), 0.0, (v + mirror) * 0.5)
+        last = minus_i((v - mirror) * 0.5)
+        zero_square, last_square = zero * zero, last * last
+        powers = jnp.where(
+            at_lane < HALF, zero_square + swap(zero_square), last_square + swap(last_square)
+        ) * pixel_scale
+        ky = spot + fold * my
+        height = jnp.where(ky >= length // 2, ky - length, ky).astype(F32)
+        kernel_real, kernel_imag = kernel_of(float(-(length // 2)), height)
+        turned = times_i(kernel_real * last + kernel_imag * times_i(last))
+        edge = ky == length // 2
+        real = jnp.where(edge, 0.0, turned) - zero
+        imag = jnp.where(edge, times_i(last), 0.0)
+        both = jnp.concatenate([real, imag], 1)
+        back = column_product(jnp.concatenate([both, each(times_i, both)], 0))
+
+        def scatter(k, carry):
+            shift = lax.rem(LANES - k, LANES)
+            for part in range(2):
+                span = slice(part * LANES, (part + 1) * LANES)
+                value = pltpu.roll(back[:, span], shift, axis=1)
+                shear[k, :, span] = jnp.where(spot == 0, value, shear[k, :, span])
+            power[k] = jnp.where(spot == 0, pltpu.roll(powers, shift, axis=1), power[k])
             return carry
 
-        lax.fori_loop(0, fold, repair, 0)
-
-    table[:LANES] = column[...]
-
-    def inverse_step(k, carry):
-        real, imag = shear[k, :, :LANES], shear[k, :, LANES:]
-        top = jnp.concatenate([real, imag], 1)
-        low = jnp.concatenate([times_i(real), times_i(imag)], 1)
-        shear[k] = dot3(table[:LANES], jnp.concatenate([top, low], 0))
-        cos, sin = table[:LANES, :LANES], table[:LANES, LANES:]
-        c, s = turns[0], turns[1]
-        table[:LANES, :LANES] = cos * c - sin * s
-        table[:LANES, LANES:] = sin * c + cos * s
-        return carry
-
-    lax.fori_loop(0, fold, inverse_step, 0)
+        lax.fori_loop(0, fold, scatter, 0)
 
     def inverse_tile(i, carry):
         take = pl.ds(pl.multiple_of(i * TILE, TILE), TILE)
+        c1, s1 = turns[0, take], turns[1, take] * sign
         for part in range(2):
             span = slice(part * LANES, (part + 1) * LANES)
-            lines_out = packed_fft([shear[k, take, span] for k in range(fold)], 1, times_i)
-            for b in range(fold):
-                shear[b, take, span] = lines_out[b]
+            c, s = c1, s1
+            held = [shear[0, take, span]]
+            for k in range(1, fold):
+                value = shear[k, take, span]
+                held.append(value * c + swap(value) * s)
+                c, s = c * c1 - s * s1, s * c1 + c * s1
+            for b, value in enumerate(packed_fft(held, 1, swap, sign)):
+                shear[b, take, span] = value
         return carry
 
     lax.fori_loop(0, LANES // TILE, inverse_tile, 0)
 
-    def give(step):
-        dest = lax.rem(me + step, devices)
-        return pltpu.make_async_remote_copy(
-            shear.at[dest], arrived.at[me], turn_send.at[step], turn_recv.at[step],
-            device_id=place(dest), device_id_type=MESH,
-        )
-
-    def got(step):
-        source = lax.rem(me + devices - step, devices)
-        return pltpu.make_async_remote_copy(
-            shear.at[source], arrived.at[source], turn_send.at[step], turn_recv.at[step],
-            device_id=place(source), device_id_type=MESH,
-        )
-
-    def give_step(step, carry):
-        give(step).start()
-        return carry
-
-    lax.fori_loop(1, devices, give_step, 0)
+    def give(dest):
+        return remote(
+            shear.at[dest], arrived.at[me], turn_send.at[dest], turn_recv.at[me], dest
+        )
+
+    def got(source):
+        return remote(
+            shear.at[source], arrived.at[source], turn_send.at[source], turn_recv.at[source],
+            source,
+        )
+
+    for turn in (2, 1, 3, 0):
+        def give_step(i, carry, turn=turn):
+            dest = lax.rem(r + i, rows) * planes + lax.rem(p + turn, planes)
+            give(dest).start()
+            return carry
+
+        lax.fori_loop(1 if turn == 0 else 0, rows, give_step, 0)
     arrived[me] = shear[me]
-
-    own_bins.wait()
 
     def bins_wait(step, carry):
         recv_bins(step).wait_recv()
@@ -500,16 +540,13 @@
 
     lax.fori_loop(1, devices, bins_wait, 0)
 
-    at_row = lax.broadcasted_iota(jnp.int32, (2 * LANES, 2 * LANES), 0)
-    at_column = lax.broadcasted_iota(jnp.int32, (2 * LANES, 2 * LANES), 1)
-    which = lax.rem(at_row // 4, 2)
     order = 4 * (at_row // 8) + lax.rem(at_row, 4)
     swapped = jnp.where(k_me == 0, 0, h_me)
     plain = lax.rem(1 - order // HALF + swapped, 2)
     origin = jnp.where((k_me == 0) & (h_me == 0), 2 * HALF, 2 * HALF - 1)
     inside = lax.rem(order, HALF)
     target = jnp.where(plain == 1, inside, HALF + lax.rem(origin - inside, HALF))
-    target = target + which * LANES
+    target = target + which_row * LANES
     table[...] = jnp.where(target == at_column, 1.0, 0.0)
 
     def bins_turn(k, carry):
@@ -527,7 +564,7 @@
 
     def band_step(k, carry):
         flipped = jnp.dot(
-            reverse_of(k), bands[lax.rem(fold - k, fold)].astype(BF16),
+            reverse_of(jnp.where(k == 0, 0, 1)), bands[lax.rem(fold - k, fold)].astype(BF16),
             preferred_element_type=F32,
         )
         band = jnp.where(lane < HALF, bands[k], flipped)
@@ -548,16 +585,12 @@
 
     def tell(step):
         dest = lax.rem(me + step, devices)
-        return pltpu.make_async_remote_copy(
-            sums_out, sums_in.at[me], sum_send.at[step], sum_recv.at[step],
-            device_id=place(dest), device_id_type=MESH,
-        )
+        return remote(sums_out, sums_in.at[me], total_send.at[step], total_recv.at[step], dest)
 
     def told(step):
         source = lax.rem(me + devices - step, devices)
-        return pltpu.make_async_remote_copy(
-            sums_out, sums_in.at[source], sum_send.at[step], sum_recv.at[step],
-            device_id=place(source), device_id_type=MESH,
+        return remote(
+            sums_out, sums_in.at[source], total_send.at[step], total_recv.at[step], source
         )
 
     def tell_step(step, carry):
@@ -566,13 +599,13 @@
 
     lax.fori_loop(1, devices, tell_step, 0)
 
-    def got_step(step, carry):
-        got(step).wait_recv()
-        return carry
-
-    lax.fori_loop(1, devices, got_step, 0)
-
-    def back_step(k, carry):
+    def back_step(i, carry):
+        k = lax.rem(me // 2 + slots - i, slots)
+        for h in range(2):
+            @pl.when(2 * k + h != me)
+            def _():
+                got(2 * k + h).wait_recv()
+
         angle = (lane * k).astype(F32) * angle_unit
         c, s = jnp.cos(angle), jnp.sin(angle)
         cos, sin = back_base[:, :LANES], back_base[:, LANES:]
@@ -616,7 +649,7 @@
     out_spectrum[...] = jnp.sum(sums_in[...], axis=0)
 
     def last_step(step, carry):
-        give(step).wait_send()
+        give(lax.rem(me + step, devices)).wait_send()
         tell(step).wait_send()
         send_bins(step).wait_send()
         return carry
@@ -624,16 +657,8 @@
     lax.fori_loop(1, devices, last_step, 0)
 
     def sent_step(dest, carry):
-        for owner in range(planes):
-            if owner > 0:
-                @pl.when(p < owner)
-                def _():
-                    up(dest, owner).wait_send()
-
-            if owner < planes - 1:
-                @pl.when(p > owner)
-                def _():
-                    down(dest, owner).wait_send()
+        for which in range(6):
+            sum_copy(which, dest).wait_send()
 
         @pl.when(dest != r)
         def _():
@@ -649,10 +674,7 @@
     devices = rows * planes
     slab, length = density.shape[1:]
     fold, blocks, slots = devices, slab // LANES, devices // 2
-    groups = LANES // fold
-    bins = spectrum_bin.reshape(LANES, fold // 2, 2, groups, fold)
-    bins = bins.transpose(4, 1, 2, 3, 0).reshape(fold, fold // 2, 2 * groups, LANES)
-    bins = bins.astype(F32)
+    middle = blocks // 2
     row_base, row_zero = row_tables(fold)
     back_base, back_zero = back_tables(fold)
     vmem = pl.BlockSpec(memory_space=pltpu.VMEM)
@@ -664,22 +686,26 @@
         pltpu.VMEM((2, min(64, slab), length), F32),
         pltpu.VMEM((slots, slab, 2 * LANES), F32),
         pltpu.VMEM((rows, planes) + chunk, F32),
-        pltpu.VMEM((rows, planes - 1) + chunk, F32),
-        pltpu.VMEM((rows, planes - 1) + chunk, F32),
+        pltpu.VMEM((rows, blocks - middle, LANES, LANES), F32),
+        pltpu.VMEM((rows, middle, LANES, LANES), F32),
+        pltpu.VMEM((rows,) + chunk, F32),
+        pltpu.VMEM((rows,) + chunk, F32),
         pltpu.VMEM((fold, LANES, LANES), F32),
         pltpu.VMEM((fold, LANES, LANES), F32),
         pltpu.VMEM((fold, LANES, 2 * LANES), F32),
         pltpu.VMEM((fold, LANES, LANES), F32),
         pltpu.VMEM((devices, LANES, 2 * LANES), F32),
-        pltpu.VMEM((devices, fold // 2, 2 * groups, LANES), F32),
+        pltpu.VMEM((length, LANES), jnp.int32),
+        pltpu.VMEM((fold, fold // 2, TILE, LANES), F32),
+        pltpu.VMEM((devices, fold // 2, TILE, LANES), F32),
         pltpu.VMEM((fold, LANES, LANES), F32),
         pltpu.VMEM((NBINS, TILE, LANES), F32),
         pltpu.VMEM((TILE, LANES), F32),
         pltpu.VMEM((devices, TILE, LANES), F32),
         pltpu.VMEM((2 * LANES, 2 * LANES), F32),
+        pltpu.VMEM((LANES, 6 * LANES), BF16),
         dma((2,)),
-        dma((rows, planes - 1)), dma((rows, planes - 1)),
-        dma((rows, planes - 1)), dma((rows, planes - 1)),
+        dma((6, rows)), dma((6, rows)),
         dma((rows,)), dma((rows,)),
         dma((devices,)), dma((devices,)), dma,
         dma((devices,)), dma((devices,)),
@@ -700,7 +726,7 @@
         ),
         name="shear",
     )(
-        density[0], lens_weight, bins,
+        density[0], lens_weight, spectrum_bin,
         row_base, row_zero, back_base, back_zero, column_table(), turn_table(length),
     )
     return real, imag, spectrum[0, :NBINS]
@@ -844,8 +870,7 @@
     count, length, width = density.shape
     return (
         count == planes
-        and planes % 2 == 0
-        and planes >= 2
+        and planes == 4
         and length == width == LANES * rows * planes
         and rows * planes == LANES // 4
     )

time: 402 us -> 302 us (0.75)
  the two profiles are of different devices: /device:TPU:25 before, /device:TPU:0 now
where the time goes in v1:
time: 302 us; the launch traced here: 301 us
  Pallas kernels  294 us (97%)
  local copies, waits for them, and re-layouts  5.77 us (2%)
    pallas_call x1, Pallas kernels, folded_device(): pl.pallas_call(functools.partial(shear_kernel, rows, planes, slab), out_s...  294 us

profile of v1, /device:TPU:0, one launch (start us, length us, event | category | flops | bytes accessed | tf_op | source)
XLA Modules:
  0.0 301.5 jit_solution(7249329493689983853)
XLA Ops:
  1.3 294.4 %shear.1 = (f32[128,4096]{1,0:T(8,128)}, f32[128,4096]{1,0:T(8,128)}, f32[8,128]{1,0:T(8,128)}) custom-call(f32[512,4096]{1,0:T(8,128)} %bitcast.3, f32[1]{0:T(128)S(6)} %copy.14.weight, s32[4096,128]{1,0:T(8,128)} %bins.1, f32[256,256]{1,0:T(8,128)} %constant.12.clone.row_base, f32[256,256]{1,0:T(8,128)} %constant.13.clone.row_zero, ...), custom_call_target="tpu_custom_call" | custom-call | tf_op jit(solution)/shard_map/shear/pallas_call | solution.py:714
  295.7 1.2 slice_bitcast_fusion
  296.9 0.0 copy-start
  296.9 3.3 %copy.15 = f32[128,4096]{1,0:T(8,128)} copy(f32[128,4096]{1,0:T(8,128)} %get-tuple-element.12) | data formatting | bytes 4194304
  300.1 0.0 copy-done
  300.2 1.3 copy.16
Async XLA Ops:
  296.9 3.3 %copy-start = (f32[128,4096]{1,0:T(8,128)S(1)}, f32[128,4096]{1,0:T(8,128)}, u32[]{:S(2)}) copy-start(f32[128,4096]{1,0:T(8,128)} %get-tuple-element.13) | copy-start | bytes 6291460

commit v2 on v1

--- a/solution.py
+++ b/solution.py
@@ -147,7 +147,7 @@
     rows, planes, slab,
     density, weight, bins, row_base, row_zero, back_base, back_zero, column, turns,
     out_real, out_imag, out_spectrum,
-    staged, folded, parts, far_low, far_high, near_low, near_high, lines, hat, shear, power,
+    staged, folded, parts, outer_inner, outer_own, outer_far, inner_outer, last_own, lines, hat, shear, power,
     arrived, bins_raw, bins_out, bins_in, bands, sums, sums_out, sums_in, table, split_column,
     stage_sem, sum_send, sum_recv, cross_send, cross_recv,
     bins_send, bins_recv, bins_load, turn_send, turn_recv, total_send, total_recv,
@@ -157,7 +157,6 @@
     length = fold * LANES
     slots = fold // 2
     blocks = slab // LANES
-    middle = blocks // 2
     pairs = planes // 2
     angle_unit = 2 * math.pi / length
     r, p = lax.axis_index("rows"), lax.axis_index("planes")
@@ -223,28 +222,36 @@
                 folded[k, put, LANES:] = spec[k][1]
             return carry
 
-        return lax.fori_loop(0, depth // TILE, tile, carry)
+        return lax.fori_loop(0, depth // TILE, tile, carry, unroll=2)
 
     lax.fori_loop(0, chunks, stage_step, 0)
-    pl.semaphore_wait(barrier, devices - 1)
-
-    first, second = pl.ds(0, middle), pl.ds(middle, blocks - middle)
-    above, below = lax.rem(p + 1, planes), lax.rem(p + planes - 1, planes)
-    across_ring = lax.rem(p + 2, planes)
+
+    side_plane = p // 2
+    end, centre = (planes - 1) * side_plane, 1 + side_plane
+    inner = planes - 1 - p
+    is_end = lax.rem(p, planes - 1) == 0
+    is_middle = lax.rem(p, planes - 1) > 0
 
     def sum_copy(which, dest):
-        owner, half, target, to = (
-            (across_ring, first, far_high.at[dest], below),
-            (across_ring, second, far_low.at[dest], above),
-            (above, first, near_low.at[dest, first], above),
-            (above, second, near_low.at[dest, second], above),
-            (below, first, near_high.at[dest, first], below),
-            (below, second, near_high.at[dest, second], below),
+        owner, target, to = (
+            (planes - 1 - centre, outer_inner, centre),
+            (centre, outer_own, centre),
+            (planes - 1 - p, outer_far, centre),
+            (inner, last_own, inner),
+            (planes - 1 - end, inner_outer, inner),
+            (end, last_own, end),
         )[which]
         return remote(
-            parts.at[dest, owner, half], target,
+            parts.at[dest, owner], target.at[dest],
             sum_send.at[which, dest], sum_recv.at[which, dest], r * planes + to,
         )
+
+    def sum_wait(which, dest):
+        target = (outer_inner, outer_own, outer_far, last_own, inner_outer, last_own)[which]
+        remote(
+            target.at[dest], target.at[dest], sum_send.at[which, dest],
+            sum_recv.at[which, dest], r * planes + lax.rem(p + 1, planes),
+        ).wait_recv()
 
     def cross(dest):
         return remote(
@@ -281,11 +288,27 @@
                 parts[dest, 2 * pair, q] = done[:, :LANES]
                 parts[dest, 2 * pair + 1, q] = done[:, LANES:]
 
-        for which in (0, 1, 2, 5):
-            sum_copy(which, dest).start()
-        return carry
-
+
+        @pl.when(is_end)
+        def _():
+            sum_copy(2, dest).start()
+
+        return carry
+
+    pl.semaphore_wait(barrier, devices - 1)
     lax.fori_loop(0, rows, row_step, 0)
+
+    def turn_of(i):
+        return lax.rem(r + 1 + i, rows)
+
+    @pl.when(is_end)
+    def _():
+        def near_step(i, carry):
+            sum_copy(0, turn_of(i)).start()
+            sum_copy(1, turn_of(i)).start()
+            return carry
+
+        lax.fori_loop(0, rows, near_step, 0)
 
     at_row = lax.broadcasted_iota(jnp.int32, (2 * LANES, 2 * LANES), 0)
     at_column = lax.broadcasted_iota(jnp.int32, (2 * LANES, 2 * LANES), 1)
@@ -303,7 +326,7 @@
         bins_out[:, k] = out.reshape(fold, TILE, LANES)
         return carry
 
-    lax.fori_loop(0, fold // 2, bins_layout, 0)
+    lax.fori_loop(0, fold // 2, bins_layout, 0, unroll=2)
     side = me // slots
 
     def class_at(owner):
@@ -324,38 +347,72 @@
             bins_out.at[0], bins_in.at[source], bins_send.at[step], bins_recv.at[step], source
         )
 
-    def relay_step(i, carry):
-        dest = lax.rem(r + 1 + i, rows)
-        sum_copy(1, dest).wait_recv()
-        parts[dest, above, second] = parts[dest, above, second] + far_low[dest]
-        sum_copy(3, dest).start()
-        sum_copy(0, dest).wait_recv()
-        parts[dest, below, first] = parts[dest, below, first] + far_high[dest]
-        sum_copy(4, dest).start()
-        return carry
-
-    lax.fori_loop(0, rows, relay_step, 0)
-
-    def bins_step(step, carry):
-        send_bins(step).start()
-        return carry
-
-    lax.fori_loop(1, devices, bins_step, 0)
-    bins_in[me] = bins_out[class_at(me)]
-
-    def owner_step(i, carry):
-        dest = lax.rem(r + 1 + i, rows)
-        for which in (2, 3, 4, 5):
-            sum_copy(which, dest).wait_recv()
-        parts[dest, p] = parts[dest, p] + near_low[dest] + near_high[dest]
-
+    def own_sum(dest):
         @pl.when(dest != r)
         def _():
             cross(dest).start()
 
-        return carry
-
-    lax.fori_loop(0, rows, owner_step, 0)
+    @pl.when(is_middle)
+    def _():
+        def far_relay(i, carry):
+            @pl.when(i < rows)
+            def _():
+                dest = turn_of(i)
+                sum_wait(2, dest)
+                owner = planes - 1 - end
+                parts[dest, owner] = parts[dest, owner] + outer_far[dest]
+                sum_copy(4, dest).start()
+
+            @pl.when(i > 0)
+            def _():
+                dest = turn_of(i - 1)
+                sum_wait(4, dest)
+                parts[dest, end] = parts[dest, end] + inner_outer[dest]
+                sum_copy(5, dest).start()
+
+            return carry
+
+        lax.fori_loop(0, rows + 1, far_relay, 0)
+
+    def bins_step(step, carry):
+        send_bins(step).start()
+        return carry
+
+    lax.fori_loop(1, devices, bins_step, 0)
+    bins_in[me] = bins_out[class_at(me)]
+
+    @pl.when(is_middle)
+    def _():
+        def near_relay(i, carry):
+            @pl.when(i < rows)
+            def _():
+                dest = turn_of(i)
+                sum_wait(0, dest)
+                parts[dest, inner] = parts[dest, inner] + outer_inner[dest]
+                sum_copy(3, dest).start()
+
+            @pl.when(i > 1)
+            def _():
+                dest = turn_of(i - 2)
+                sum_wait(1, dest)
+                sum_wait(3, dest)
+                parts[dest, p] = parts[dest, p] + outer_own[dest] + last_own[dest]
+                own_sum(dest)
+
+            return carry
+
+        lax.fori_loop(0, rows + 2, near_relay, 0)
+
+    @pl.when(is_end)
+    def _():
+        def end_step(i, carry):
+            dest = turn_of(i)
+            sum_wait(5, dest)
+            parts[dest, p] = parts[dest, p] + last_own[dest]
+            own_sum(dest)
+            return carry
+
+        lax.fori_loop(0, rows, end_step, 0)
 
     def own_step(q, carry):
         lines[r * blocks + q] = parts[r, p, q]
@@ -380,7 +437,7 @@
             c, s = c * c1 - s * s1, s * c1 + c * s1
         return carry
 
-    lax.fori_loop(0, LANES // TILE, column_tile, 0)
+    lax.fori_loop(0, LANES // TILE, column_tile, 0, unroll=2)
 
     k_me, h_me = me // 2, lax.rem(me, 2)
     index = lax.rem(lane, HALF)
@@ -440,7 +497,7 @@
         shear[2 * j + 1] = back[:, 2 * LANES:]
         return carry
 
-    lax.fori_loop(0, fold // 2, column_step, 0)
+    lax.fori_loop(0, fold // 2, column_step, 0, unroll=2)
 
     def reverse_of(wrap):
         return jnp.where(lax.rem(LANES - wrap - my, LANES) == at_lane, 1.0, 0.0).astype(BF16)
@@ -452,7 +509,7 @@
         def gather(k, held):
             return jnp.where(spot == k, pltpu.roll(hat[k], k, axis=1), held)
 
-        v = lax.fori_loop(0, fold, gather, jnp.zeros((LANES, LANES), F32))
+        v = lax.fori_loop(0, fold, gather, jnp.zeros((LANES, LANES), F32), unroll=2)
         high, low = split(v)
 
         def moved(wrap):
@@ -495,7 +552,7 @@
             power[k] = jnp.where(spot == 0, pltpu.roll(powers, shift, axis=1), power[k])
             return carry
 
-        lax.fori_loop(0, fold, scatter, 0)
+        lax.fori_loop(0, fold, scatter, 0, unroll=2)
 
     def inverse_tile(i, carry):
         take = pl.ds(pl.multiple_of(i * TILE, TILE), TILE)
@@ -512,7 +569,7 @@
                 shear[b, take, span] = value
         return carry
 
-    lax.fori_loop(0, LANES // TILE, inverse_tile, 0)
+    lax.fori_loop(0, LANES // TILE, inverse_tile, 0, unroll=2)
 
     def give(dest):
         return remote(
@@ -527,8 +584,7 @@
 
     for turn in (2, 1, 3, 0):
         def give_step(i, carry, turn=turn):
-            dest = lax.rem(r + i, rows) * planes + lax.rem(p + turn, planes)
-            give(dest).start()
+            give(lax.rem(r + i, rows) * planes + lax.rem(p + turn, planes)).start()
             return carry
 
         lax.fori_loop(1 if turn == 0 else 0, rows, give_step, 0)
@@ -559,7 +615,7 @@
         bands[2 * k + 1] = out[:, LANES:]
         return carry
 
-    lax.fori_loop(0, fold // 2, bins_turn, 0)
+    lax.fori_loop(0, fold // 2, bins_turn, 0, unroll=2)
     sums[...] = jnp.zeros_like(sums)
 
     def band_step(k, carry):
@@ -625,7 +681,7 @@
         folded[k, :2 * LANES] = dot3(jnp.concatenate(left, 0), table[...])
         return carry
 
-    lax.fori_loop(0, slots, back_step, 0)
+    lax.fori_loop(0, slots, back_step, 0, unroll=2)
 
     for part, out in enumerate((out_real, out_imag)):
         def back_tile(i, carry, part=part, out=out):
@@ -639,7 +695,7 @@
                 out[put, b * LANES:(b + 1) * LANES] = value
             return carry
 
-        lax.fori_loop(0, LANES // TILE, back_tile, 0)
+        lax.fori_loop(0, LANES // TILE, back_tile, 0, unroll=2)
 
     def told_step(step, carry):
         told(step).wait_recv()
@@ -657,8 +713,15 @@
     lax.fori_loop(1, devices, last_step, 0)
 
     def sent_step(dest, carry):
-        for which in range(6):
-            sum_copy(which, dest).wait_send()
+        @pl.when(is_end)
+        def _():
+            for which in (0, 1, 2):
+                sum_copy(which, dest).wait_send()
+
+        @pl.when(is_middle)
+        def _():
+            for which in (3, 4, 5):
+                sum_copy(which, dest).wait_send()
 
         @pl.when(dest != r)
         def _():
@@ -674,7 +737,6 @@
     devices = rows * planes
     slab, length = density.shape[1:]
     fold, blocks, slots = devices, slab // LANES, devices // 2
-    middle = blocks // 2
     row_base, row_zero = row_tables(fold)
     back_base, back_zero = back_tables(fold)
     vmem = pl.BlockSpec(memory_space=pltpu.VMEM)
@@ -686,8 +748,9 @@
         pltpu.VMEM((2, min(64, slab), length), F32),
         pltpu.VMEM((slots, slab, 2 * LANES), F32),
         pltpu.VMEM((rows, planes) + chunk, F32),
-        pltpu.VMEM((rows, blocks - middle, LANES, LANES), F32),
-        pltpu.VMEM((rows, middle, LANES, LANES), F32),
+        pltpu.VMEM((rows,) + chunk, F32),
+        pltpu.VMEM((rows,) + chunk, F32),
+        pltpu.VMEM((rows,) + chunk, F32),
         pltpu.VMEM((rows,) + chunk, F32),
         pltpu.VMEM((rows,) + chunk, F32),
         pltpu.VMEM((fold, LANES, LANES), F32),

time: 302 us -> 287 us (0.950)
  Pallas kernels: 294 us -> 280 us
    pallas_call x1, Pallas kernels: 294 us -> 280 us  [folded_device(): pl.pallas_call(functools.partial(shear_kernel, rows, planes, slab), out_s...]
where the time goes in v2:
time: 287 us
  Pallas kernels  280 us (98%)
  local copies, waits for them, and re-layouts  5.77 us (2%)
    pallas_call x1, Pallas kernels, folded_device(): pl.pallas_call(functools.partial(shear_kernel, rows, planes, slab), out_s...  280 us

profile of v2, /device:TPU:0, one launch (start us, length us, event | category | flops | bytes accessed | tf_op | source)
XLA Modules:
  0.0 286.9 jit_solution(8383830694712539311)
XLA Ops:
  1.3 279.8 %shear.1 = (f32[128,4096]{1,0:T(8,128)}, f32[128,4096]{1,0:T(8,128)}, f32[8,128]{1,0:T(8,128)}) custom-call(f32[512,4096]{1,0:T(8,128)} %bitcast.3, f32[1]{0:T(128)S(6)} %copy.14.weight, s32[4096,128]{1,0:T(8,128)} %bins.1, f32[256,256]{1,0:T(8,128)} %constant.12.clone.row_base, f32[256,256]{1,0:T(8,128)} %constant.13.clone.row_zero, ...), custom_call_target="tpu_custom_call" | custom-call | tf_op jit(solution)/shard_map/shear/pallas_call | solution.py:777
  281.1 1.2 slice_bitcast_fusion
  282.3 0.0 copy-start
  282.3 3.3 %copy.15 = f32[128,4096]{1,0:T(8,128)} copy(f32[128,4096]{1,0:T(8,128)} %get-tuple-element.12) | data formatting | bytes 4194304
  285.6 0.0 copy-done
  285.6 1.3 copy.16
Async XLA Ops:
  282.3 3.3 %copy-start = (f32[128,4096]{1,0:T(8,128)S(1)}, f32[128,4096]{1,0:T(8,128)}, u32[]{:S(2)}) copy-start(f32[128,4096]{1,0:T(8,128)} %get-tuple-element.13) | copy-start | bytes 6291460

commit v3 on v2

--- a/solution.py
+++ b/solution.py
@@ -378,7 +378,10 @@
         send_bins(step).start()
         return carry
 
-    lax.fori_loop(1, devices, bins_step, 0)
+    @pl.when(is_middle)
+    def _():
+        lax.fori_loop(1, devices, bins_step, 0)
+
     bins_in[me] = bins_out[class_at(me)]
 
     @pl.when(is_middle)
@@ -582,12 +585,22 @@
             source,
         )
 
-    for turn in (2, 1, 3, 0):
-        def give_step(i, carry, turn=turn):
-            give(lax.rem(r + i, rows) * planes + lax.rem(p + turn, planes)).start()
+    def give_plane(plane, begin):
+        def give_step(i, carry):
+            give(lax.rem(r + i, rows) * planes + plane).start()
             return carry
 
-        lax.fori_loop(1 if turn == 0 else 0, rows, give_step, 0)
+        lax.fori_loop(begin, rows, give_step, 0)
+
+    give_plane(lax.rem(p + 2, planes), 0)
+    give_plane(planes - 1 - p, 0)
+
+    @pl.when(is_end)
+    def _():
+        lax.fori_loop(1, devices, bins_step, 0)
+
+    give_plane(p + 1 - 2 * lax.rem(p, 2), 0)
+    give_plane(p, 1)
     arrived[me] = shear[me]
 
     def bins_wait(step, carry):
@@ -656,7 +669,8 @@
     lax.fori_loop(1, devices, tell_step, 0)
 
     def back_step(i, carry):
-        k = lax.rem(me // 2 + slots - i, slots)
+        near = lax.rem(side_plane + i // rows, pairs)
+        k = lax.rem(r + 2 * rows - i, rows) * pairs + near
         for h in range(2):
             @pl.when(2 * k + h != me)
             def _():

time: 287 us -> 283 us (0.986)
  Pallas kernels: 280 us -> 276 us
    pallas_call x1, Pallas kernels: 280 us -> 276 us  [folded_device(): pl.pallas_call(functools.partial(shear_kernel, rows, planes, slab), out_s...]
where the time goes in v3:
time: 283 us
  Pallas kernels  276 us (98%)
  local copies, waits for them, and re-layouts  5.77 us (2%)
    pallas_call x1, Pallas kernels, folded_device(): pl.pallas_call(functools.partial(shear_kernel, rows, planes, slab), out_s...  276 us

profile of v3, /device:TPU:0, one launch (start us, length us, event | category | flops | bytes accessed | tf_op | source)
XLA Modules:
  0.0 282.6 jit_solution(17499728454748888382)
XLA Ops:
  1.3 275.6 %shear.1 = (f32[128,4096]{1,0:T(8,128)}, f32[128,4096]{1,0:T(8,128)}, f32[8,128]{1,0:T(8,128)}) custom-call(f32[512,4096]{1,0:T(8,128)} %bitcast.3, f32[1]{0:T(128)S(6)} %copy.14.weight, s32[4096,128]{1,0:T(8,128)} %bins.1, f32[256,256]{1,0:T(8,128)} %constant.12.clone.row_base, f32[256,256]{1,0:T(8,128)} %constant.13.clone.row_zero, ...), custom_call_target="tpu_custom_call" | custom-call | tf_op jit(solution)/shard_map/shear/pallas_call | solution.py:791
  276.9 1.2 slice_bitcast_fusion
  278.1 0.0 copy-start
  278.1 3.3 %copy.15 = f32[128,4096]{1,0:T(8,128)} copy(f32[128,4096]{1,0:T(8,128)} %get-tuple-element.12) | data formatting | bytes 4194304
  281.3 0.0 copy-done
  281.3 1.3 copy.16
Async XLA Ops:
  278.1 3.3 %copy-start = (f32[128,4096]{1,0:T(8,128)S(1)}, f32[128,4096]{1,0:T(8,128)}, u32[]{:S(2)}) copy-start(f32[128,4096]{1,0:T(8,128)} %get-tuple-element.13) | copy-start | bytes 6291460

commit v4 on v3

--- a/solution.py
+++ b/solution.py
@@ -267,7 +267,7 @@
 
     at_a = lax.broadcasted_iota(jnp.int32, (LANES, LANES), 0)
 
-    def row_step(i, carry):
+    def row_products(i):
         dest = lax.rem(r + 1 + i, rows)
         for pair in range(pairs):
             k = dest * pairs + pair
@@ -289,17 +289,23 @@
                 parts[dest, 2 * pair + 1, q] = done[:, LANES:]
 
 
+    def turn_of(i):
+        return lax.rem(r + 1 + i, rows)
+
+    def row_step(i, carry):
         @pl.when(is_end)
         def _():
-            sum_copy(2, dest).start()
-
-        return carry
-
+            sum_copy(2, turn_of(i)).start()
+
+        @pl.when(i + 1 < rows)
+        def _():
+            row_products(i + 1)
+
+        return carry
+
+    row_products(jnp.int32(0))
     pl.semaphore_wait(barrier, devices - 1)
     lax.fori_loop(0, rows, row_step, 0)
-
-    def turn_of(i):
-        return lax.rem(r + 1 + i, rows)
 
     @pl.when(is_end)
     def _():
@@ -593,12 +599,12 @@
         lax.fori_loop(begin, rows, give_step, 0)
 
     give_plane(lax.rem(p + 2, planes), 0)
-    give_plane(planes - 1 - p, 0)
 
     @pl.when(is_end)
     def _():
         lax.fori_loop(1, devices, bins_step, 0)
 
+    give_plane(planes - 1 - p, 0)
     give_plane(p + 1 - 2 * lax.rem(p, 2), 0)
     give_plane(p, 1)
     arrived[me] = shear[me]

time: 283 us -> 282 us (level)
  no operation moved by 1% of the time
where the time goes in v4:
time: 282 us
  Pallas kernels  275 us (98%)
  local copies, waits for them, and re-layouts  5.77 us (2%)
    pallas_call x1, Pallas kernels, folded_device(): pl.pallas_call(functools.partial(shear_kernel, rows, planes, slab), out_s...  275 us

profile of v4, /device:TPU:0, one launch (start us, length us, event | category | flops | bytes accessed | tf_op | source)
XLA Modules:
  0.0 282.1 jit_solution(3532774620222020454)
XLA Ops:
  1.3 275.1 %shear.1 = (f32[128,4096]{1,0:T(8,128)}, f32[128,4096]{1,0:T(8,128)}, f32[8,128]{1,0:T(8,128)}) custom-call(f32[512,4096]{1,0:T(8,128)} %bitcast.3, f32[1]{0:T(128)S(6)} %copy.14.weight, s32[4096,128]{1,0:T(8,128)} %bins.1, f32[256,256]{1,0:T(8,128)} %constant.12.clone.row_base, f32[256,256]{1,0:T(8,128)} %constant.13.clone.row_zero, ...), custom_call_target="tpu_custom_call" | custom-call | tf_op jit(solution)/shard_map/shear/pallas_call | solution.py:797
  276.4 1.2 slice_bitcast_fusion
  277.5 0.0 copy-start
  277.5 3.3 %copy.15 = f32[128,4096]{1,0:T(8,128)} copy(f32[128,4096]{1,0:T(8,128)} %get-tuple-element.12) | data formatting | bytes 4194304
  280.8 0.0 copy-done
  280.8 1.3 copy.16
Async XLA Ops:
  277.5 3.3 %copy-start = (f32[128,4096]{1,0:T(8,128)S(1)}, f32[128,4096]{1,0:T(8,128)}, u32[]{:S(2)}) copy-start(f32[128,4096]{1,0:T(8,128)} %get-tuple-element.13) | copy-start | bytes 6291460
